TPU v7x, 32 devices: a whole 2x2x4 slice. The times are simulated.
32 devices in a mesh: pr: 4 (over y, x), pc: 8 (over z, core).
Axes of the slice: x: 2, y: 2, z: 4, core: 2. Of those that a mesh axis runs over, the one named last changes fastest.
Arguments:
- pair_state: bfloat16 [96, 96, 128], P('pr', 'pc'), may hold values from -6 to 6
- left_weight: bfloat16 [128, 128], replicated, may hold values from -0.5 to 0.5
- right_weight: bfloat16 [128, 128], replicated, may hold values from -0.5 to 0.5
- mid_gain: float32 [128], replicated, may hold values from 0.25 to 1.75
- out_weight: bfloat16 [128, 128], replicated, may hold values from -0.5 to 0.5
- out_gate: bfloat16 [128, 128], replicated, may hold values from -0.5 to 0.5
Outputs:
- pair_update: bfloat16 [96, 96, 128], P('pr', 'pc')
All inputs are finite; a program needn't handle non-finite values.
Results may differ from a plain program's by a relative error of at most 0.012.
Values may be sent and summed in bfloat16 or wider, within the bound.
A program may use at most 128 MiB of HBM per device.

v0:
```python
import jax
import jax.numpy as jnp
from jax import lax
from jax.sharding import PartitionSpec as P


def scale_channels(values, channel_gain):
    centred = values - jnp.mean(values, axis=-1, keepdims=True)
    return (
        centred
        * lax.rsqrt(jnp.mean(centred * centred, axis=-1, keepdims=True) + 1e-05)
        * channel_gain
    )


def project_pair(pair_in, left_weight, right_weight):
    left = jnp.einsum("ijc,cd->ijd", pair_in, left_weight, preferred_element_type=jnp.float32)
    right = jnp.einsum("ijc,cd->ijd", pair_in, right_weight, preferred_element_type=jnp.float32)
    return (pair_in, left.astype(jnp.bfloat16), right.astype(jnp.bfloat16))


def close_update(mixed, ready, mid_gain, out_weight, out_gate):
    scaled = scale_channels(mixed.astype(jnp.float32), mid_gain).astype(jnp.bfloat16)
    scaled = lax.optimization_barrier(scaled)
    gate = jax.nn.sigmoid(
        jnp.einsum("ijc,cd->ijd", ready, out_gate, preferred_element_type=jnp.float32)
    )
    return (
        jnp.einsum("ijd,dc->ijc", scaled, out_weight, preferred_element_type=jnp.float32) * gate
    ).astype(jnp.bfloat16)


def body(pair_state, left_weight, right_weight, mid_gain, out_weight, out_gate):
    ready, left, right = project_pair(pair_state, left_weight, right_weight)
    count = pair_state.shape[0] * lax.axis_size("pr")
    left_lines, right_lines = (
        lax.all_to_all(left, "pr", split_axis=2, concat_axis=0, tiled=True),
        lax.all_to_all(right, "pr", split_axis=2, concat_axis=0, tiled=True),
    )
    strip = jnp.einsum(
        "kid,kjd->ijd",
        lax.all_gather(left_lines, "pc", axis=1, tiled=True),
        right_lines,
        preferred_element_type=jnp.float32,
    )
    strip = (strip * count ** (-0.5)).astype(jnp.bfloat16)
    mixed = lax.all_to_all(strip, "pr", split_axis=0, concat_axis=2, tiled=True)
    return close_update(mixed, ready, mid_gain, out_weight, out_gate)


def solution(mesh):
    placed = (P("pr", "pc", None), P(), P(), P(), P(), P())
    return jax.shard_map(
        body, mesh=mesh, in_specs=placed, out_specs=P("pr", "pc", None), check_vma=False
    )
```

profile of v0, /device:TPU:0, one launch (start us, length us, event | category | flops | bytes accessed | tf_op | source)
XLA Modules:
  0.0 52.5 jit_solution(6551884356601724737)
XLA Ops:
  0.0 0.0 copy-start
  0.0 0.9 %copy-done = bf16[24,12,128]{2,0,1:T(8,128)(2,1)S(1)} copy-done((bf16[24,12,128]{2,0,1:T(8,128)(2,1)S(1)}, bf16[24,12,128]{2,0,1:T(8,128)(2,1)}, u32[]{:S(2)}) %copy-start) | copy-done | bytes 73752
  0.9 0.9 %convolution_convert_fusion.1 = bf16[24,12,128]{2,0,1:T(8,128)(2,1)S(1)} fusion(bf16[24,12,128]{2,0,1:T(8,128)(2,1)S(1)} %copy-done, bf16[128,128]{1,0:T(8,128)(2,1)} %param.8), kind=kOutput, calls=%fused_computation.10 | convolution fusion | flops 9474048 | bytes 180224 | tf_op jit(solution)/shard_map/ijc,cd->ijd/dot_general | solution.py:18
  1.8 0.4 copy.39
  2.3 1.1 %reshape.28 = bf16[4,2,4608]{2,1,0:T(2,128)(2,1)} reshape(bf16[128,12,24]{2,1,0:T(8,128)(2,1)S(1)} %bitcast.44) | data formatting | bytes 147456
  3.4 0.0 copy-start.1
  3.4 5.3 %all-to-all-start = ((bf16[4,2,4608]{2,1,0:T(2,128)(2,1)}), bf16[4,2,4608]{2,1,0:T(2,128)(2,1)S(1)}, u32[]{:S(2)}, u32[]{:S(2)}) async-start(bf16[4,2,4608]{2,1,0:T(2,128)(2,1)} %reshape.28), calls=%async_computation | async-start | bytes 147456 | tf_op jit(solution)/shard_map/all_to_all | solution.py:38
  8.7 0.0 copy-done.1
  8.7 0.2 convolution_convert_fusion
  8.9 0.4 copy.41
  9.3 1.1 %reshape.26 = bf16[4,2,4608]{2,1,0:T(2,128)(2,1)} reshape(bf16[128,12,24]{2,1,0:T(8,128)(2,1)S(1)} %bitcast.45) | data formatting | bytes 147456
  10.5 3.1 %all-to-all-done = bf16[4,2,4608]{2,1,0:T(2,128)(2,1)S(1)} async-done(((bf16[4,2,4608]{2,1,0:T(2,128)(2,1)}), bf16[4,2,4608]{2,1,0:T(2,128)(2,1)S(1)}, u32[]{:S(2)}, u32[]{:S(2)}) %all-to-all-start) | async-done | bytes 73760 | tf_op jit(solution)/shard_map/all_to_all | solution.py:38
  13.6 3.3 %all-to-all-start.1 = ((bf16[4,2,4608]{2,1,0:T(2,128)(2,1)}), bf16[4,2,4608]{2,1,0:T(2,128)(2,1)S(1)}, u32[]{:S(2)}, u32[]{:S(2)}) async-start(bf16[4,2,4608]{2,1,0:T(2,128)(2,1)} %reshape.26), calls=%async_computation.1 | async-start | bytes 147456 | tf_op jit(solution)/shard_map/all_to_all | solution.py:37
  16.9 0.6 %reshape.29 = bf16[128,12,24]{2,1,0:T(8,128)(2,1)S(1)} reshape(bf16[4,2,4608]{2,1,0:T(2,128)(2,1)S(1)} %all-to-all-done) | data formatting | bytes 147456
  17.5 0.3 copy.55
  17.8 0.2 all_to_all.36
  18.0 3.7 %all-to-all-done.1 = bf16[4,2,4608]{2,1,0:T(2,128)(2,1)S(1)} async-done(((bf16[4,2,4608]{2,1,0:T(2,128)(2,1)}), bf16[4,2,4608]{2,1,0:T(2,128)(2,1)S(1)}, u32[]{:S(2)}, u32[]{:S(2)}) %all-to-all-start.1) | async-done | bytes 73760 | tf_op jit(solution)/shard_map/all_to_all | solution.py:37
  21.7 0.6 %reshape.27 = bf16[128,12,24]{2,1,0:T(8,128)(2,1)S(1)} reshape(bf16[4,2,4608]{2,1,0:T(2,128)(2,1)S(1)} %all-to-all-done.1) | data formatting | bytes 147456
  22.3 0.3 copy.54
  22.6 0.2 all_to_all.40
  22.9 16.5 %all_gather.3 = bf16[96,96,32]{0,2,1:T(8,128)(2,1)S(1)} all-gather(bf16[96,12,32]{0,2,1:T(8,128)(2,1)S(1)} %all_to_all.40), channel_id=1, replica_groups=mesh['pr'=4,'pc'=8] {'pc'}, dimensions={1}, use_global_device_ids=true | all-gather | bytes 663552 | tf_op jit(solution)/shard_map/all_gather | solution.py:42
  39.4 0.5 fusion.5
  39.9 0.4 copy.45
  40.3 0.3 reshape.30
  40.6 7.2 %all_to_all.45 = bf16[4,2,4608]{2,1,0:T(2,128)(2,1)S(1)} all-to-all(bf16[4,2,4608]{2,1,0:T(2,128)(2,1)S(1)} %reshape.30), channel_id=1, replica_groups=mesh['pr'=4,'pc'=8] {'pr'}, dimensions={0} | all-to-all | bytes 147456 | tf_op jit(solution)/shard_map/all_to_all | solution.py:47
  47.8 0.2 reshape.31
  48.1 0.3 copy.46
  48.4 0.4 reshape.21
  48.8 0.1 bitcast_reduce_fusion
  48.9 0.3 multiply_reduce_fusion
  49.2 0.3 copy.47
  49.5 0.0 copy-start.3
  49.5 0.3 reshape.19
  49.8 0.4 copy-done.3
  50.2 0.0 copy-start.2
  50.2 0.1 multiply_convert_fusion
  50.3 0.6 %copy-done.2 = bf16[128,128]{1,0:T(8,128)(2,1)S(1)} copy-done((bf16[128,128]{1,0:T(8,128)(2,1)S(1)}, bf16[128,128]{1,0:T(8,128)(2,1)}, u32[]{:S(2)}) %copy-start.2) | copy-done | bytes 32792
  50.9 0.0 copy-start.4
  50.9 0.2 fusion.10
  51.1 0.6 %copy-done.4 = bf16[128,128]{1,0:T(8,128)(2,1)S(1)} copy-done((bf16[128,128]{1,0:T(8,128)(2,1)S(1)}, bf16[128,128]{1,0:T(8,128)(2,1)}, u32[]{:S(2)}) %copy-start.4) | copy-done | bytes 32792
  51.7 0.8 %fusion.6 = bf16[24,12,128]{2,0,1:T(8,128)(2,1)} fusion(f32[24,12,128]{2,0,1:T(8,128)S(1)} %fusion.10, bf16[24,12,128]{2,0,1:T(8,128)(2,1)S(1)} %copy-done, bf16[128,128]{1,0:T(8,128)(2,1)S(1)} %copy-done.4), kind=kOutput, calls=%fused_computation.8 | convolution fusion | flops 9621504 | bytes 327680 | tf_op jit(solution)/shard_map/ijc,cd->ijd/dot_general | solution.py:26
  (2 shorter events, 0.0 us)
Async XLA Ops:
  0.0 0.9 %copy-start = (bf16[24,12,128]{2,0,1:T(8,128)(2,1)S(1)}, bf16[24,12,128]{2,0,1:T(8,128)(2,1)}, u32[]{:S(2)}) copy-start(bf16[24,12,128]{2,0,1:T(8,128)(2,1)} %param.6) | copy-start | bytes 221188
  3.4 5.3 %copy-start.1 = (bf16[128,128]{1,0:T(8,128)(2,1)S(1)}, bf16[128,128]{1,0:T(8,128)(2,1)}, u32[]{:S(2)}) copy-start(bf16[128,128]{1,0:T(8,128)(2,1)} %param.7) | copy-start | bytes 98308
  3.4 10.2 %all-to-all-start = ((bf16[4,2,4608]{2,1,0:T(2,128)(2,1)}), bf16[4,2,4608]{2,1,0:T(2,128)(2,1)S(1)}, u32[]{:S(2)}, u32[]{:S(2)}) async-start(bf16[4,2,4608]{2,1,0:T(2,128)(2,1)} %reshape.28), calls=%async_computation | async-start | bytes 147456 | tf_op jit(solution)/shard_map/all_to_all | solution.py:38
  13.6 8.1 %all-to-all-start.1 = ((bf16[4,2,4608]{2,1,0:T(2,128)(2,1)}), bf16[4,2,4608]{2,1,0:T(2,128)(2,1)S(1)}, u32[]{:S(2)}, u32[]{:S(2)}) async-start(bf16[4,2,4608]{2,1,0:T(2,128)(2,1)} %reshape.26), calls=%async_computation.1 | async-start | bytes 147456 | tf_op jit(solution)/shard_map/all_to_all | solution.py:37
  49.5 0.7 %copy-start.3 = (f32[128]{0:T(128)S(1)}, f32[128]{0:T(128)}, u32[]{:S(2)}) copy-start(f32[128]{0:T(128)} %param.9) | copy-start | bytes 1540
  50.2 0.8 %copy-start.2 = (bf16[128,128]{1,0:T(8,128)(2,1)S(1)}, bf16[128,128]{1,0:T(8,128)(2,1)}, u32[]{:S(2)}) copy-start(bf16[128,128]{1,0:T(8,128)(2,1)} %param.10) | copy-start | bytes 98308
  50.9 0.8 %copy-start.4 = (bf16[128,128]{1,0:T(8,128)(2,1)S(1)}, bf16[128,128]{1,0:T(8,128)(2,1)}, u32[]{:S(2)}) copy-start(bf16[128,128]{1,0:T(8,128)(2,1)} %param.11) | copy-start | bytes 98308
where the time goes:
time: 53.2 us; the launch traced here: 52.5 us
  blocking collectives  23.7 us (45%)
  local copies, waits for them, and re-layouts  10.1 us (19%)
  starting transfers between devices  8.61 us (16%)
  waiting for transfers between devices  6.78 us (13%)
  matrix products  2.61 us (5%)
  other arithmetic  0.54 us (1%)
    all_gather x1, blocking collectives, body(): lax.all_gather(left_lines, 'pc', axis=1, tiled=True)  16.5 us
    all_to_all x1, blocking collectives, body(): mixed = lax.all_to_all(strip, 'pr', split_axis=0, concat_axis=2, tiled=True)  7.24 us
    unnamed x16, local copies, waits for them, and re-layouts  6.51 us
    all_to_all x1, starting transfers between devices, body(): lax.all_to_all(right, 'pr', split_axis=2, concat_axis=0, tiled=True)  5.32 us
    all_to_all x1, waiting for transfers between devices, body(): lax.all_to_all(left, 'pr', split_axis=2, concat_axis=0, tiled=True)  3.68 us
    all_to_all x1, starting transfers between devices, body(): lax.all_to_all(left, 'pr', split_axis=2, concat_axis=0, tiled=True)  3.29 us
    all_to_all x1, waiting for transfers between devices, body(): lax.all_to_all(right, 'pr', split_axis=2, concat_axis=0, tiled=True)  3.1 us
  transfers between devices with their start and end apart: 2, of which 2 were waited for; matrix products, arithmetic and copies ran while one was open for 5% of the time, Pallas kernels for 0%

commit v1 on v0

--- a/solution.py
+++ b/solution.py
@@ -33,9 +33,16 @@
 def body(pair_state, left_weight, right_weight, mid_gain, out_weight, out_gate):
     ready, left, right = project_pair(pair_state, left_weight, right_weight)
     count = pair_state.shape[0] * lax.axis_size("pr")
+
+    def scan_layers_all(mine):
+        return jnp.concatenate(
+            lax.all_to_all(jnp.stack(jnp.split(mine, lax.axis_size("pr"), 2), axis=0), "pr", 0, 0),
+            0,
+        )
+
     left_lines, right_lines = (
         lax.all_to_all(left, "pr", split_axis=2, concat_axis=0, tiled=True),
-        lax.all_to_all(right, "pr", split_axis=2, concat_axis=0, tiled=True),
+        scan_layers_all(right),
     )
     strip = jnp.einsum(
         "kid,kjd->ijd",

time: 53.2 us -> 52.7 us (level)
  local copies, waits for them, and re-layouts: 10.1 us -> 9.13 us
    unnamed x16, local copies, waits for them, and re-layouts: 6.51 us -> 5.84 us
    reshape x0 -> x2, local copies, waits for them, and re-layouts: none -> 0.58 us  [scan_layers_all(): jnp.concatenate(lax.all_to_all(jnp.stack(jnp.split(mine, lax.axis_size('p...]
where the time goes in v1:
time: 52.7 us; the launch traced here: 52 us
  blocking collectives  23.7 us (45%)
  local copies, waits for them, and re-layouts  9.13 us (17%)
  starting transfers between devices  8.61 us (16%)
  waiting for transfers between devices  7.15 us (14%)
  matrix products  2.61 us (5%)
  other arithmetic  0.63 us (1%)
    all_gather x1, blocking collectives, body(): lax.all_gather(left_lines, 'pc', axis=1, tiled=True)  16.5 us
    all_to_all x1, blocking collectives, body(): mixed = lax.all_to_all(strip, 'pr', split_axis=0, concat_axis=2, tiled=True)  7.24 us
    unnamed x16, local copies, waits for them, and re-layouts  5.84 us
    all_to_all x1, starting transfers between devices, scan_layers_all(): lax.all_to_all(jnp.stack(jnp.split(mine, lax.axis_size('pr'), 2), axis=0)...  5.32 us
    all_to_all x1, waiting for transfers between devices, body(): lax.all_to_all(left, 'pr', split_axis=2, concat_axis=0, tiled=True)  4.04 us
    all_to_all x1, starting transfers between devices, body(): lax.all_to_all(left, 'pr', split_axis=2, concat_axis=0, tiled=True)  3.29 us
    all_to_all x1, waiting for transfers between devices, scan_layers_all(): lax.all_to_all(jnp.stack(jnp.split(mine, lax.axis_size('pr'), 2), axis=0)...  3.11 us
  transfers between devices with their start and end apart: 2, of which 2 were waited for; matrix products, arithmetic and copies ran while one was open for 5% of the time, Pallas kernels for 0%

profile of v1, /device:TPU:0, one launch (start us, length us, event | category | flops | bytes accessed | tf_op | source)
XLA Modules:
  0.0 52.0 jit_solution(6563115257097415228)
XLA Ops:
  0.0 0.0 copy-start
  0.0 0.9 %copy-done = bf16[24,12,128]{2,0,1:T(8,128)(2,1)S(1)} copy-done((bf16[24,12,128]{2,0,1:T(8,128)(2,1)S(1)}, bf16[24,12,128]{2,0,1:T(8,128)(2,1)}, u32[]{:S(2)}) %copy-start) | copy-done | bytes 73752
  0.9 0.9 %convolution_convert_fusion.1 = bf16[24,12,128]{2,0,1:T(8,128)(2,1)S(1)} fusion(bf16[24,12,128]{2,0,1:T(8,128)(2,1)S(1)} %copy-done, bf16[128,128]{1,0:T(8,128)(2,1)} %param.8), kind=kOutput, calls=%fused_computation.10 | convolution fusion | flops 9474048 | bytes 180224 | tf_op jit(solution)/shard_map/ijc,cd->ijd/dot_general | solution.py:18
  1.8 0.1 slice_bitcast_fusion.3
  2.0 0.1 fusion.13
  2.0 0.9 %reshape.31 = bf16[4,2,4608]{2,1,0:T(2,128)(2,1)} reshape(bf16[4,12,24,32]{3,2,1,0:T(8,128)(2,1)S(1)} %fusion.13) | data formatting | bytes 147456
  2.9 0.0 copy-start.1
  2.9 5.3 %all-to-all-start = ((bf16[4,2,4608]{2,1,0:T(2,128)(2,1)}), bf16[4,2,4608]{2,1,0:T(2,128)(2,1)S(1)}, u32[]{:S(2)}, u32[]{:S(2)}) async-start(bf16[4,2,4608]{2,1,0:T(2,128)(2,1)} %reshape.31), calls=%async_computation | async-start | bytes 147456 | tf_op jit(solution)/shard_map/all_to_all | solution.py:39
  8.3 0.0 copy-done.1
  8.3 0.2 convolution_convert_fusion
  8.4 0.4 copy.37
  8.9 1.1 %reshape.33 = bf16[4,2,4608]{2,1,0:T(2,128)(2,1)} reshape(bf16[128,12,24]{2,1,0:T(8,128)(2,1)S(1)} %bitcast.49) | data formatting | bytes 147456
  10.0 3.1 %all-to-all-done = bf16[4,2,4608]{2,1,0:T(2,128)(2,1)S(1)} async-done(((bf16[4,2,4608]{2,1,0:T(2,128)(2,1)}), bf16[4,2,4608]{2,1,0:T(2,128)(2,1)S(1)}, u32[]{:S(2)}, u32[]{:S(2)}) %all-to-all-start) | async-done | bytes 73760 | tf_op jit(solution)/shard_map/all_to_all | solution.py:39
  13.1 3.3 %all-to-all-start.1 = ((bf16[4,2,4608]{2,1,0:T(2,128)(2,1)}), bf16[4,2,4608]{2,1,0:T(2,128)(2,1)S(1)}, u32[]{:S(2)}, u32[]{:S(2)}) async-start(bf16[4,2,4608]{2,1,0:T(2,128)(2,1)} %reshape.33), calls=%async_computation.1 | async-start | bytes 147456 | tf_op jit(solution)/shard_map/all_to_all | solution.py:44
  16.4 0.2 reshape.32
  16.6 0.4 copy.44
  17.0 0.2 reshape.30
  17.2 4.0 %all-to-all-done.1 = bf16[4,2,4608]{2,1,0:T(2,128)(2,1)S(1)} async-done(((bf16[4,2,4608]{2,1,0:T(2,128)(2,1)}), bf16[4,2,4608]{2,1,0:T(2,128)(2,1)S(1)}, u32[]{:S(2)}, u32[]{:S(2)}) %all-to-all-start.1) | async-done | bytes 73760 | tf_op jit(solution)/shard_map/all_to_all | solution.py:44
  21.3 0.6 %reshape.34 = bf16[128,12,24]{2,1,0:T(8,128)(2,1)S(1)} reshape(bf16[4,2,4608]{2,1,0:T(2,128)(2,1)S(1)} %all-to-all-done.1) | data formatting | bytes 147456
  21.9 0.3 copy.49
  22.2 0.2 all_to_all.27
  22.4 16.5 %all_gather.3 = bf16[96,96,32]{0,2,1:T(8,128)(2,1)S(1)} all-gather(bf16[96,12,32]{0,2,1:T(8,128)(2,1)S(1)} %all_to_all.27), channel_id=1, replica_groups=mesh['pr'=4,'pc'=8] {'pc'}, dimensions={1}, use_global_device_ids=true | all-gather | bytes 663552 | tf_op jit(solution)/shard_map/all_gather | solution.py:49
  38.9 0.5 fusion.5
  39.4 0.4 copy.41
  39.8 0.3 reshape.35
  40.1 7.2 %all_to_all.32 = bf16[4,2,4608]{2,1,0:T(2,128)(2,1)S(1)} all-to-all(bf16[4,2,4608]{2,1,0:T(2,128)(2,1)S(1)} %reshape.35), channel_id=1, replica_groups=mesh['pr'=4,'pc'=8] {'pr'}, dimensions={0} | all-to-all | bytes 147456 | tf_op jit(solution)/shard_map/all_to_all | solution.py:54
  47.4 0.2 reshape.36
  47.6 0.3 copy.42
  47.9 0.4 reshape.25
  48.3 0.1 bitcast_reduce_fusion
  48.4 0.3 multiply_reduce_fusion
  48.7 0.3 copy.43
  49.0 0.0 copy-start.3
  49.0 0.3 reshape.23
  49.3 0.4 copy-done.3
  49.7 0.0 copy-start.2
  49.7 0.1 multiply_convert_fusion
  49.8 0.6 %copy-done.2 = bf16[128,128]{1,0:T(8,128)(2,1)S(1)} copy-done((bf16[128,128]{1,0:T(8,128)(2,1)S(1)}, bf16[128,128]{1,0:T(8,128)(2,1)}, u32[]{:S(2)}) %copy-start.2) | copy-done | bytes 32792
  50.4 0.0 copy-start.4
  50.4 0.2 fusion.9
  50.6 0.6 %copy-done.4 = bf16[128,128]{1,0:T(8,128)(2,1)S(1)} copy-done((bf16[128,128]{1,0:T(8,128)(2,1)S(1)}, bf16[128,128]{1,0:T(8,128)(2,1)}, u32[]{:S(2)}) %copy-start.4) | copy-done | bytes 32792
  51.2 0.8 %fusion.6 = bf16[24,12,128]{2,0,1:T(8,128)(2,1)} fusion(f32[24,12,128]{2,0,1:T(8,128)S(1)} %fusion.9, bf16[24,12,128]{2,0,1:T(8,128)(2,1)S(1)} %copy-done, bf16[128,128]{1,0:T(8,128)(2,1)S(1)} %copy-done.4), kind=kOutput, calls=%fused_computation.8 | convolution fusion | flops 9621504 | bytes 327680 | tf_op jit(solution)/shard_map/ijc,cd->ijd/dot_general | solution.py:26
  (2 shorter events, 0.0 us)
Async XLA Ops:
  0.0 0.9 %copy-start = (bf16[24,12,128]{2,0,1:T(8,128)(2,1)S(1)}, bf16[24,12,128]{2,0,1:T(8,128)(2,1)}, u32[]{:S(2)}) copy-start(bf16[24,12,128]{2,0,1:T(8,128)(2,1)} %param.6) | copy-start | bytes 221188
  2.9 5.3 %copy-start.1 = (bf16[128,128]{1,0:T(8,128)(2,1)S(1)}, bf16[128,128]{1,0:T(8,128)(2,1)}, u32[]{:S(2)}) copy-start(bf16[128,128]{1,0:T(8,128)(2,1)} %param.7) | copy-start | bytes 98308
  2.9 10.2 %all-to-all-start = ((bf16[4,2,4608]{2,1,0:T(2,128)(2,1)}), bf16[4,2,4608]{2,1,0:T(2,128)(2,1)S(1)}, u32[]{:S(2)}, u32[]{:S(2)}) async-start(bf16[4,2,4608]{2,1,0:T(2,128)(2,1)} %reshape.31), calls=%async_computation | async-start | bytes 147456 | tf_op jit(solution)/shard_map/all_to_all | solution.py:39
  13.1 8.1 %all-to-all-start.1 = ((bf16[4,2,4608]{2,1,0:T(2,128)(2,1)}), bf16[4,2,4608]{2,1,0:T(2,128)(2,1)S(1)}, u32[]{:S(2)}, u32[]{:S(2)}) async-start(bf16[4,2,4608]{2,1,0:T(2,128)(2,1)} %reshape.33), calls=%async_computation.1 | async-start | bytes 147456 | tf_op jit(solution)/shard_map/all_to_all | solution.py:44
  49.0 0.7 %copy-start.3 = (f32[128]{0:T(128)S(1)}, f32[128]{0:T(128)}, u32[]{:S(2)}) copy-start(f32[128]{0:T(128)} %param.9) | copy-start | bytes 1540
  49.7 0.8 %copy-start.2 = (bf16[128,128]{1,0:T(8,128)(2,1)S(1)}, bf16[128,128]{1,0:T(8,128)(2,1)}, u32[]{:S(2)}) copy-start(bf16[128,128]{1,0:T(8,128)(2,1)} %param.10) | copy-start | bytes 98308
  50.4 0.8 %copy-start.4 = (bf16[128,128]{1,0:T(8,128)(2,1)S(1)}, bf16[128,128]{1,0:T(8,128)(2,1)}, u32[]{:S(2)}) copy-start(bf16[128,128]{1,0:T(8,128)(2,1)} %param.11) | copy-start | bytes 98308
